TPU v7x, 32 devices: a whole 2x2x4 slice. The times are simulated.
32 devices in a mesh: groups: 2 (over y), expert: 4 (over z), tensor: 4 (over x, core).
Axes of the slice: x: 2, y: 2, z: 4, core: 2. Of those that a mesh axis runs over, the one named last changes fastest.
Arguments:
- tokens: bfloat16 [256, 4096], P(('groups', 'expert'), 'tensor'), parts along dimension 0, may hold values from -6 to 6
- expert_ids: int32 [256, 8], P(('groups', 'expert')), parts along dimension 0, may hold values from 0 to 63, all different within a row; in each aligned block of 32 rows (0 to 31, 32 to 63, ...) at most 8 rows name the same one
- gate_fixed: int32 [256, 8], P(('groups', 'expert')), parts along dimension 0, may hold values from 1 to 65535
- w_gate: bfloat16 [64, 4096, 768], P('expert', None, 'tensor'), may hold values from -0.09375 to 0.09375
- w_up: bfloat16 [64, 4096, 768], P('expert', None, 'tensor'), may hold values from -0.09375 to 0.09375
- w_down: bfloat16 [64, 768, 4096], P('expert', 'tensor'), may hold values from -0.21875 to 0.21875
Outputs:
- mixed: bfloat16 [256, 4096], P(('groups', 'expert'), 'tensor'), parts along dimension 0
There are 2 independent parts, one for each index of `groups`. A program takes and returns all parts, laid end to end along the dimension named above; an argument that names none is the same for every part. Nothing has to cross between parts.
Inputs may be any that keep to these rules, and one draw needn't show every extreme that they name: `expert_ids`: each row names 8 different experts. Within the 32 rows of one index of the expert axis no expert is named more than 8 times, and in every draw some expert is named exactly 8 times in some such block.
All inputs are finite; a program needn't handle non-finite values.
Results may differ from a plain program's by a relative error of at most 0.014.
Values may be sent and summed in bfloat16 or wider, within the bound.
No kernel may reach another device: no remote copies, remote signals or barrier semaphores. Data moves between devices by JAX's collectives and lax.ppermute only.
A program may use at most 128 MiB of HBM per device.

v0:
```python
import jax
import jax.numpy as jnp
from jax import lax
from jax.sharding import PartitionSpec as P

CAP = 8


def expert_block(slot_rows, w_gate, w_up, w_down):
    gate_proj = jnp.einsum("gekd,edf->gekf", slot_rows, w_gate, preferred_element_type=jnp.float32)
    up_proj = jnp.einsum("gekd,edf->gekf", slot_rows, w_up, preferred_element_type=jnp.float32)
    hidden = (jax.nn.silu(gate_proj) * up_proj).astype(jnp.bfloat16)
    partial_value = jnp.einsum("gekf,efd->gekd", hidden, w_down, preferred_element_type=jnp.float32)
    summed = lax.psum_scatter(
        partial_value.astype(jnp.bfloat16), "tensor", scatter_dimension=3, tiled=True
    )
    return lax.all_to_all(summed, "expert", split_axis=0, concat_axis=0, tiled=True)


def on_device(tokens, expert_ids, gate_fixed, w_gate, w_up, w_down):
    tok_rows, per_token = expert_ids.shape
    local_experts = w_gate.shape[0]
    devices_e = lax.axis_size("expert")
    experts = local_experts * devices_e
    capacity = CAP
    flat_ids = expert_ids.reshape(-1)
    pick_count = tok_rows * per_token
    onehot = (flat_ids[:, None] == jnp.arange(experts, dtype=jnp.int32)[None, :]).astype(jnp.int32)
    before = jnp.cumsum(onehot, axis=0) - onehot
    slot_rank = jnp.sum(before * onehot, axis=1)
    slot_index = flat_ids * capacity + slot_rank
    owner_row = jnp.arange(pick_count, dtype=jnp.int32) // per_token
    slot_token = jnp.full((experts * capacity,), tok_rows, jnp.int32).at[slot_index].set(owner_row)
    padded = jnp.concatenate([tokens, jnp.zeros((1, tokens.shape[1]), tokens.dtype)], axis=0)
    returned = expert_block(
        lax.all_gather(
            lax.all_to_all(
                padded[slot_token].reshape(devices_e, local_experts, capacity, tokens.shape[1]),
                "expert",
                split_axis=0,
                concat_axis=0,
                tiled=True,
            ),
            "tensor",
            axis=3,
            tiled=True,
        ),
        w_gate,
        w_up,
        w_down,
    )
    flat_returned = returned.reshape(experts * capacity, returned.shape[3])
    picked = flat_returned[slot_index].reshape(tok_rows, per_token, returned.shape[3])
    weights = gate_fixed.astype(jnp.float32)
    gate_share = weights / jnp.sum(weights, axis=1, keepdims=True)
    mixed_out = jnp.einsum("tk,tkf->tf", gate_share, picked.astype(jnp.float32))
    return mixed_out.astype(jnp.bfloat16)


def solution(mesh):
    placed = (
        P(("groups", "expert"), "tensor"),
        P(("groups", "expert"), None),
        P(("groups", "expert"), None),
        P("expert", None, "tensor"),
        P("expert", None, "tensor"),
        P("expert", "tensor", None),
    )
    return jax.shard_map(
        on_device,
        mesh=mesh,
        in_specs=placed,
        out_specs=P(("groups", "expert"), "tensor"),
        check_vma=False,
    )
```

profile of v0, /device:TPU:0, one launch (start us, length us, event | category | flops | bytes accessed | tf_op | source)
XLA Modules:
  0.0 207.7 jit_solution(213641463679312116)
XLA Ops:
  6.5 0.0 all-gather.2.cloned.1.call-start
  6.5 0.8 copy.14
  7.3 0.1 eq.29
  7.4 0.1 eq.25
  7.5 0.7 broadcast_multiply_fusion
  8.2 0.6 reduce-window.6
  8.8 0.2 slice_reduce_fusion
  9.0 0.1 copy.13
  9.1 0.1 mul.28
  9.2 0.1 fusion.28
  9.3 1.4 scatter_custom_fusion
  10.7 0.8 concatenate.3
  11.6 2.0 gather_fusion
  13.7 31.9 %all_to_all.10 = bf16[4,16,8,1024]{3,2,1,0:T(8,128)(2,1)S(1)} all-to-all(bf16[4,16,8,1024]{3,2,1,0:T(8,128)(2,1)S(1)} %bitcast.73), channel_id=1, replica_groups=mesh['groups'=2,'expert'=4,'tensor'=4] {'expert'}, dimensions={0} | all-to-all | bytes 2097152 | tf_op jit(solution)/shard_map/all_to_all | solution.py:37
  45.5 1.1 copy.17
  46.6 0.0 all-gather.2.cloned.1.call-update
  46.6 0.0 reduce-scatter.2.cloned.1.call-start
  46.7 33.7 %all-gather.2.cloned.1.call-done = bf16[4,16,8,4096]{3,2,0,1:T(8,128)(2,1)} async-done(((bf16[4,16,8,1024]{3,2,0,1:T(8,128)(2,1)}), bf16[4,16,8,4096]{3,2,0,1:T(8,128)(2,1)}) %all-gather.2.cloned.1.call-update) | async-done | bytes 4194320 | tf_op jit(solution)/shard_map/all_gather | solution.py:36
  80.3 13.2 %fusion.12 = f32[4,16,8,192]{3,2,0,1:T(8,128)S(1)} fusion(bf16[4,16,8,4096]{3,2,0,1:T(8,128)(2,1)} %all-gather.2.cloned.1.call-done, bf16[16,4096,192]{1,2,0:T(8,128)(2,1)} %param.9), kind=kOutput, calls=%fused_computation.11 | convolution fusion | flops 805306368 | bytes 29753344 | tf_op jit(solution)/shard_map/gekd,edf->gekf/dot_general | solution.py:10
  93.6 13.4 %fusion.21 = bf16[4,16,8,192]{3,2,0,1:T(8,128)(2,1)S(1)} fusion(bf16[4,16,8,4096]{3,2,0,1:T(8,128)(2,1)} %all-gather.2.cloned.1.call-done, bf16[16,4096,192]{1,2,0:T(8,128)(2,1)} %param.10, f32[4,16,8,192]{3,2,0,1:T(8,128)S(1)} %fusion.12), kind=kOutput, calls=%fused_computation.14 | convolution fusion | flops 805896192 | bytes 29949952 | tf_op jit(solution)/shard_map/gekd,edf->gekf/dot_general | solution.py:11
  107.0 0.0 copy-start
  107.0 14.6 %fusion.9 = bf16[4,16,8,4096]{3,2,0,1:T(8,128)(2,1)} fusion(bf16[4,16,8,192]{3,2,0,1:T(8,128)(2,1)S(1)} %fusion.21, bf16[16,192,4096]{2,1,0:T(8,128)(2,1)} %param.11), kind=kOutput, calls=%fused_computation.10 | convolution fusion | flops 807403520 | bytes 29556736 | tf_op jit(solution)/shard_map/gekf,efd->gekd/dot_general | solution.py:13
  121.7 0.0 reduce-scatter.2.cloned.1.call-update
  121.7 44.6 %reduce-scatter.2.cloned.1.call-done = bf16[4,16,8,1024]{3,2,0,1:T(8,128)(2,1)} async-done(((bf16[4,16,8,4096]{3,2,0,1:T(8,128)(2,1)}), bf16[4,16,8,1024]{3,2,0,1:T(8,128)(2,1)}) %reduce-scatter.2.cloned.1.call-update) | async-done | bytes 1048592 | tf_op jit(solution)/shard_map/reduce_scatter | solution.py:14
  166.3 2.3 %copy.18 = bf16[4,16,8,1024]{3,2,1,0:T(8,128)(2,1)} copy(bf16[4,16,8,1024]{3,2,0,1:T(8,128)(2,1)} %reduce-scatter.2.cloned.1.call-done) | data formatting | bytes 2097152 | tf_op jit(solution)/shard_map/reduce_scatter | solution.py:14
  168.6 4.6 %all-to-all-start.1 = ((bf16[4,16,8,1024]{3,2,1,0:T(8,128)(2,1)}), bf16[4,16,8,1024]{3,2,1,0:T(8,128)(2,1)S(1)}, u32[]{:S(2)}, u32[]{:S(2)}) async-start(bf16[4,16,8,1024]{3,2,1,0:T(8,128)(2,1)} %copy.18), calls=%async_computation.2 | async-start | bytes 2097152 | tf_op jit(solution)/shard_map/all_to_all | solution.py:17
  173.2 0.0 copy-done
  173.2 0.1 copy.22
  173.3 25.4 %all-to-all-done.1 = bf16[4,16,8,1024]{3,2,1,0:T(8,128)(2,1)S(1)} async-done(((bf16[4,16,8,1024]{3,2,1,0:T(8,128)(2,1)}), bf16[4,16,8,1024]{3,2,1,0:T(8,128)(2,1)S(1)}, u32[]{:S(2)}, u32[]{:S(2)}) %all-to-all-start.1) | async-done | bytes 1048608 | tf_op jit(solution)/shard_map/all_to_all | solution.py:17
  198.7 1.2 gather_fusion.1
  199.9 0.3 fusion.24
  200.2 0.7 copy.27
  (10 shorter events, 0.1 us)
Async XLA Ops:
  6.5 73.8 %all-gather.2.cloned.1.call-start = ((), (), s32[]{:S(2)}) async-start(), calls=%async_computation.3 | async-start | bytes 5242880 | tf_op jit(solution)/shard_map/all_gather | solution.py:36
  46.6 119.6 %reduce-scatter.2.cloned.1.call-start = ((), (), s32[]{:S(2)}) async-start(), calls=%async_computation.4 | async-start | bytes 5242880 | tf_op jit(solution)/shard_map/reduce_scatter | solution.py:14
  107.0 66.2 %copy-start = (s32[32,8]{0,1:T(8,128)S(1)}, s32[32,8]{0,1:T(8,128)}, u32[]{:S(2)}) copy-start(s32[32,8]{0,1:T(8,128)} %param.8) | copy-start | bytes 3076
  168.6 30.1 %all-to-all-start.1 = ((bf16[4,16,8,1024]{3,2,1,0:T(8,128)(2,1)}), bf16[4,16,8,1024]{3,2,1,0:T(8,128)(2,1)S(1)}, u32[]{:S(2)}, u32[]{:S(2)}) async-start(bf16[4,16,8,1024]{3,2,1,0:T(8,128)(2,1)} %copy.18), calls=%async_computation.2 | async-start | bytes 2097152 | tf_op jit(solution)/shard_map/all_to_all | solution.py:17
Sparse Core Ops, SparseCore 0:
  46.7 33.5 all-gather.1
  121.8 44.4 reduce-scatter.1
where the time goes:
time: 208 us
  waiting for transfers between devices  104 us (50%)
  matrix products  41.6 us (20%)
  blocking collectives  31.9 us (15%)
  between operations  13.5 us (6%)
  local copies, waits for them, and re-layouts  10.9 us (5%)
  starting transfers between devices  4.64 us (2%)
    reduce_scatter x1, waiting for transfers between devices, expert_block(): lax.psum_scatter(partial_value.astype(jnp.bfloat16), 'tensor', scatter_di...  44.6 us
    all_gather x1, waiting for transfers between devices, on_device(): lax.all_gather(lax.all_to_all(padded[slot_token].reshape(devices_e, local...  33.7 us
    all_to_all x1, blocking collectives, on_device(): lax.all_to_all(padded[slot_token].reshape(devices_e, local_experts, capac...  31.9 us
    all_to_all x1, waiting for transfers between devices, expert_block(): lax.all_to_all(summed, 'expert', split_axis=0, concat_axis=0, tiled=True)  25.4 us
    dot_general x1, matrix products, expert_block(): jnp.einsum('gekf,efd->gekd', hidden, w_down, preferred_element_type=jnp.f...  14.6 us
    dot_general x1, matrix products, expert_block(): jnp.einsum('gekd,edf->gekf', slot_rows, w_up, preferred_element_type=jnp....  13.4 us
    dot_general x1, matrix products, expert_block(): jnp.einsum('gekd,edf->gekf', slot_rows, w_gate, preferred_element_type=jn...  13.2 us
    all_to_all x1, starting transfers between devices, expert_block(): lax.all_to_all(summed, 'expert', split_axis=0, concat_axis=0, tiled=True)  4.6 us
  transfers between devices with their start and end apart: 3, of which 3 were waited for; matrix products, arithmetic and copies ran while one was open for 0% of the time, Pallas kernels for 0%

commit v1 on v0

v1 whole, which is shorter than its diff:
```python
import jax
import jax.numpy as jnp
from jax import lax
from jax.sharding import PartitionSpec as P


def swap(value, axis, step):
    count = lax.axis_size(axis)
    return lax.ppermute(value, axis, [(i, i ^ step) for i in range(count)])


def gather_rows(value, axis):
    return jnp.concatenate([value] + [swap(value, axis, j) for j in range(1, lax.axis_size(axis))], axis=0)


def scatter_rows(value, axis):
    count = lax.axis_size(axis)
    rows = value.shape[0] // count
    total = value[:rows]
    for j in range(1, count):
        block = value[j * rows:(j + 1) * rows].astype(jnp.bfloat16)
        total = total + swap(block, axis, j).astype(jnp.float32)
    return total


def on_device(tokens, expert_ids, gate_fixed, w_gate, w_up, w_down):
    per_token = expert_ids.shape[1]
    local_experts, model, units = w_gate.shape
    width = tokens.shape[1]
    devices_e = lax.axis_size("expert")
    devices_t = lax.axis_size("tensor")
    place_e = lax.axis_index("expert")
    place_t = lax.axis_index("tensor")
    few = devices_e <= 8

    routing = jnp.concatenate([expert_ids, gate_fixed], axis=1)
    if few:
        own = gather_rows(tokens, "expert")
        routing = gather_rows(routing, "expert")
    else:
        own = lax.all_gather(tokens, "expert", axis=0, tiled=True)
        routing = lax.all_gather(routing, "expert", axis=0, tiled=True)
    rows = own.shape[0]

    parts = {0: own}
    bit = devices_t >> 1
    while bit:
        for j in list(parts):
            parts[j ^ bit] = swap(parts[j], "tensor", bit)
        bit >>= 1

    ids = routing[:, :per_token]
    weights = routing[:, per_token:].astype(jnp.float32)
    gate_share = weights / jnp.sum(weights, axis=1, keepdims=True)
    mine = place_e * local_experts + jnp.arange(local_experts, dtype=jnp.int32)
    chosen = jnp.sum(
        jnp.where(ids.T[None, :, :] == mine[:, None, None], gate_share.T[None, :, :], 0.0), axis=1
    )

    gate_rows = jnp.swapaxes(w_gate, 1, 2).reshape(local_experts * units, model)
    up_rows = jnp.swapaxes(w_up, 1, 2).reshape(local_experts * units, model)
    down_rows = w_down.reshape(local_experts * units, model)

    def project(matrix):
        total = None
        for j in sorted(parts):
            piece = lax.dynamic_slice_in_dim(matrix, (place_t ^ j) * width, width, axis=1)
            term = lax.dot_general(
                piece, parts[j], (((1,), (1,)), ((), ())), preferred_element_type=jnp.float32
            )
            total = term if total is None else total + term
        return total

    gate_proj = project(gate_rows)
    up_proj = project(up_rows)
    hidden = (jax.nn.silu(gate_proj) * up_proj).reshape(local_experts, units, rows)
    hidden = (hidden * chosen[:, None, :]).astype(jnp.bfloat16).reshape(local_experts * units, rows)

    def down(j):
        piece = lax.dynamic_slice_in_dim(down_rows, (place_t ^ j) * width, width, axis=1)
        return lax.dot_general(hidden, piece, (((0,), (0,)), ((), ())), preferred_element_type=jnp.float32)

    sums = {j: down(j) for j in sorted(parts, reverse=True)}
    bit = 1
    while bit < devices_t:
        for j in sorted(sums, reverse=True):
            if j & bit:
                sums[j ^ bit] = sums[j ^ bit] + swap(sums.pop(j).astype(jnp.bfloat16), "tensor", bit).astype(jnp.float32)
        bit <<= 1
    if few:
        mixed = scatter_rows(sums[0], "expert")
    else:
        mixed = lax.psum_scatter(sums[0].astype(jnp.bfloat16), "expert", scatter_dimension=0, tiled=True)
    return mixed.astype(jnp.bfloat16)


def solution(mesh):
    placed = (
        P(("groups", "expert"), "tensor"),
        P(("groups", "expert"), None),
        P(("groups", "expert"), None),
        P("expert", None, "tensor"),
        P("expert", None, "tensor"),
        P("expert", "tensor", None),
    )
    return jax.shard_map(
        on_device,
        mesh=mesh,
        in_specs=placed,
        out_specs=P(("groups", "expert"), "tensor"),
        check_vma=False,
    )
```

time: 208 us -> 84.6 us (0.41)
  waiting for transfers between devices: 104 us -> 20.7 us
  blocking collectives: 31.9 us -> 0 us
  starting transfers between devices: 4.64 us -> 18.4 us
  between operations: 13.5 us -> 0.31 us
  local copies, waits for them, and re-layouts: 10.9 us -> 2.3 us
    reduce_scatter x1 -> x0, waiting for transfers between devices: 44.6 us -> none  [expert_block(): lax.psum_scatter(partial_value.astype(jnp.bfloat16), 'tensor', scatter_di...]
    all_gather x1 -> x0, waiting for transfers between devices: 33.7 us -> none  [on_device(): lax.all_gather(lax.all_to_all(padded[slot_token].reshape(devices_e, local...]
    all_to_all x1 -> x0, blocking collectives: 31.9 us -> none  [on_device(): lax.all_to_all(padded[slot_token].reshape(devices_e, local_experts, capac...]
    all_to_all x1 -> x0, waiting for transfers between devices: 25.4 us -> none  [expert_block(): lax.all_to_all(summed, 'expert', split_axis=0, concat_axis=0, tiled=True)]
    ppermute x0 -> x15, waiting for transfers between devices: none -> 20.7 us  [swap(): return lax.ppermute(value, axis, [(i, i ^ step) for i in range(count)])]
    ppermute x0 -> x15, starting transfers between devices: none -> 18.4 us  [swap(): return lax.ppermute(value, axis, [(i, i ^ step) for i in range(count)])]
    all_to_all x1 -> x0, starting transfers between devices: 4.6 us -> none  [expert_block(): lax.all_to_all(summed, 'expert', split_axis=0, concat_axis=0, tiled=True)]
    gather x2 -> x0, local copies, waits for them, and re-layouts: 3.22 us -> none  [the longest x1 2.05 us: on_device(): padded[slot_token]]
  transfers between devices with their start and end apart: 3 -> 15, of which waited for: 3 -> 6; matrix products, arithmetic and copies ran while one was open for 0% -> 29% of each run, Pallas kernels for 0% -> 0%
where the time goes in v1:
time: 84.6 us; the launch traced here: 84.3 us
  matrix products  41.7 us (49%)
  waiting for transfers between devices  20.7 us (24%)
  starting transfers between devices  18.4 us (22%)
  local copies, waits for them, and re-layouts  2.3 us (3%)
  other arithmetic  0.97 us (1%)
    dot_general x8, matrix products, project(): lax.dot_general(piece, parts[j], (((1,), (1,)), ((), ())), preferred_elem...  37.7 us
    ppermute x15, waiting for transfers between devices, swap(): return lax.ppermute(value, axis, [(i, i ^ step) for i in range(count)])  20.7 us
    ppermute x15, starting transfers between devices, swap(): return lax.ppermute(value, axis, [(i, i ^ step) for i in range(count)])  18.4 us
    dot_general x4, matrix products, down(): lax.dot_general(hidden, piece, (((0,), (0,)), ((), ())), preferred_elemen...  4.03 us
  transfers between devices with their start and end apart: 15, of which 6 were waited for; matrix products, arithmetic and copies ran while one was open for 29% of the time, Pallas kernels for 0%

profile of v1, /device:TPU:0, one launch (start us, length us, event | category | flops | bytes accessed | tf_op | source)
XLA Modules:
  0.0 84.3 jit_solution(7389381248176025606)
XLA Ops:
  0.0 3.1 %collective-permute-start = (bf16[32,1024]{1,0:T(8,128)(2,1)}, bf16[32,1024]{1,0:T(8,128)(2,1)S(1)}, u32[]{:S(2)}, u32[]{:S(2)}) collective-permute-start(bf16[32,1024]{1,0:T(8,128)(2,1)} %param.6), channel_id=1, source_target_pairs={{0,4},{4,0},{8,12},{12,8},{1,5},{5,1},{9,13},{13,9},{2,6},{6,2},{1... | collective-permute-start | bytes 196616 | tf_op jit(solution)/shard_map/ppermute | solution.py:9
  3.1 2.6 %collective-permute-start.1 = (bf16[32,1024]{1,0:T(8,128)(2,1)}, bf16[32,1024]{1,0:T(8,128)(2,1)S(1)}, u32[]{:S(2)}, u32[]{:S(2)}) collective-permute-start(bf16[32,1024]{1,0:T(8,128)(2,1)} %param.6), channel_id=1, source_target_pairs={{0,8},{4,12},{8,0},{12,4},{1,9},{5,13},{9,1},{13,5},{2,10},{6,14},... | collective-permute-start | bytes 196616 | tf_op jit(solution)/shard_map/ppermute | solution.py:9
  5.6 0.7 constant_dynamic-update-slice_fusion.5
  6.3 0.7 constant_dynamic-update-slice_fusion.4
  7.0 0.4 collective-permute-start.6
  7.5 0.0 collective-permute-start.7
  7.5 3.9 %collective-permute-start.8 = (s32[32,16]{0,1:T(8,128)S(1)}, s32[32,16]{0,1:T(8,128)S(1)}, u32[]{:S(2)}, u32[]{:S(2)}) collective-permute-start(s32[32,16]{0,1:T(8,128)S(1)} %constant_dynamic-update-slice_fusion.4), channel_id=1, source_target_pairs={{0,12},{4,8},{8,4},{12,0},{1,13},{5,9},{9,5},{13,1},{2,14},{6,10},... | collective-permute-start | bytes 6152 | tf_op jit(solution)/shard_map/ppermute | solution.py:9
  11.4 0.8 %constant_dynamic-update-slice_fusion.3 = bf16[128,1024]{1,0:T(8,128)(2,1)S(1)} fusion(bf16[32,1024]{1,0:T(8,128)(2,1)} %param.6), kind=kLoop, calls=%fused_computation.44 | loop fusion | bytes 131072
  12.3 0.0 collective-permute-done.6
  12.3 0.1 collective-permute-start.2
  12.3 0.0 collective-permute-done.7
  12.4 0.9 %collective-permute-done.8 = s32[32,16]{0,1:T(8,128)S(1)} collective-permute-done((s32[32,16]{0,1:T(8,128)S(1)}, s32[32,16]{0,1:T(8,128)S(1)}, u32[]{:S(2)}, u32[]{:S(2)}) %collective-permute-start.8) | collective-permute-done | bytes 2080 | tf_op jit(solution)/shard_map/ppermute | solution.py:9
  13.2 0.1 pad_add_fusion
  13.3 0.0 collective-permute-done
  13.3 0.0 collective-permute-done.1
  13.4 5.2 %collective-permute-done.2 = bf16[32,1024]{1,0:T(8,128)(2,1)S(1)} collective-permute-done((bf16[32,1024]{1,0:T(8,128)(2,1)}, bf16[32,1024]{1,0:T(8,128)(2,1)S(1)}, u32[]{:S(2)}, u32[]{:S(2)}) %collective-permute-start.2) | collective-permute-done | bytes 65568 | tf_op jit(solution)/shard_map/ppermute | solution.py:9
  18.6 1.5 %collective-permute-start.4 = (bf16[128,1024]{1,0:T(8,128)(2,1)S(1)}, bf16[128,1024]{1,0:T(8,128)(2,1)S(1)}, u32[]{:S(2)}, u32[]{:S(2)}) collective-permute-start(bf16[128,1024]{1,0:T(8,128)(2,1)S(1)} %constant_dynamic-update-slice_fusion), channel_id=1, source_target_pairs={{0,2},{1,3},{2,0},{3,1},{4,6},{5,7},{6,4},{7,5},{8,10},{9,11},{10,... | collective-permute-start | bytes 786440 | tf_op jit(solution)/shard_map/ppermute | solution.py:9
  20.1 0.1 select_reduce_fusion
  20.2 0.1 collective-permute-start.3
  20.3 4.7 %collective-permute-done.4 = bf16[128,1024]{1,0:T(8,128)(2,1)S(1)} collective-permute-done((bf16[128,1024]{1,0:T(8,128)(2,1)S(1)}, bf16[128,1024]{1,0:T(8,128)(2,1)S(1)}, u32[]{:S(2)}, u32[]{:S(2)}) %collective-permute-start.4) | collective-permute-done | bytes 262176 | tf_op jit(solution)/shard_map/ppermute | solution.py:9
  25.0 4.6 %fusion.18 = f32[3072,128]{1,0:T(8,128)S(1)} fusion(bf16[128,1024]{1,0:T(8,128)(2,1)S(1)} %collective-permute-done.4, bf16[3072,4096]{1,0:T(8,128)(2,1)} %bitcast.37, s32[]{:T(128)S(6)} %select_n.26), kind=kOutput, calls=%fused_computation.18 | convolution fusion | flops 805306368 | bytes 8126468 | tf_op jit(solution)/shard_map/dot_general | solution.py:68
  29.6 0.0 collective-permute-done.3
  29.6 4.6 %fusion.20 = f32[3072,128]{1,0:T(8,128)S(1)} fusion(bf16[128,1024]{1,0:T(8,128)(2,1)S(1)} %collective-permute-done.3, bf16[3072,4096]{1,0:T(8,128)(2,1)} %bitcast.38, s32[]{:T(128)S(6)} %select_n.13), kind=kOutput, calls=%fused_computation.20 | convolution fusion | flops 805306368 | bytes 8126468 | tf_op jit(solution)/shard_map/dot_general | solution.py:68
  34.2 4.6 %fusion.39 = f32[3072,128]{1,0:T(8,128)S(1)} fusion(f32[3072,128]{1,0:T(8,128)S(1)} %fusion.18, f32[3072,128]{1,0:T(8,128)S(1)} %fusion.20, bf16[128,1024]{1,0:T(8,128)(2,1)S(1)} %constant_dynamic-update-slice_fusion, bf16[3072,4096]{1,0:T(8,128)(2,1)} %bitcast.39, s32[]{:T(128)S(6)} %select_n.12), kind=kOutput, calls=%fused_computation.29 | convolution fusion | flops 806092800 | bytes 11272196 | tf_op jit(solution)/shard_map/dot_general | solution.py:68
  38.8 0.1 collective-permute-start.5
  38.8 0.0 slice-start
  38.9 0.0 slice-start.1
  38.9 4.7 %fusion.10 = f32[3072,128]{1,0:T(8,128)S(1)} fusion(bf16[128,1024]{1,0:T(8,128)(2,1)S(1)} %collective-permute-done.4, bf16[3072,4096]{1,0:T(8,128)(2,1)} %bitcast.33, s32[]{:T(128)S(6)} %select_n.26), kind=kOutput, calls=%fused_computation.10 | convolution fusion | flops 805306368 | bytes 8126468 | tf_op jit(solution)/shard_map/dot_general | solution.py:68
  43.6 0.0 slice-start.2
  43.6 4.7 %fusion.12 = f32[3072,128]{1,0:T(8,128)S(1)} fusion(bf16[128,1024]{1,0:T(8,128)(2,1)S(1)} %collective-permute-done.3, bf16[3072,4096]{1,0:T(8,128)(2,1)} %bitcast.34, s32[]{:T(128)S(6)} %select_n.13), kind=kOutput, calls=%fused_computation.12 | convolution fusion | flops 805306368 | bytes 8126468 | tf_op jit(solution)/shard_map/dot_general | solution.py:68
  48.4 0.0 slice-start.3
  48.4 4.7 %fusion.36 = f32[3072,128]{1,0:T(8,128)S(1)} fusion(f32[3072,128]{1,0:T(8,128)S(1)} %fusion.10, f32[3072,128]{1,0:T(8,128)S(1)} %fusion.12, bf16[128,1024]{1,0:T(8,128)(2,1)S(1)} %constant_dynamic-update-slice_fusion, bf16[3072,4096]{1,0:T(8,128)(2,1)} %bitcast.35, s32[]{:T(128)S(6)} %select_n.12), kind=kOutput, calls=%fused_computation.28 | convolution fusion | flops 806092800 | bytes 11272196 | tf_op jit(solution)/shard_map/dot_general | solution.py:68
  53.1 0.0 slice-start.4
  53.1 0.0 collective-permute-done.5
  53.2 4.9 %fusion.27 = f32[3072,128]{1,0:T(8,128)S(1)} fusion(f32[3072,128]{1,0:T(8,128)S(1)} %fusion.39, bf16[128,1024]{1,0:T(8,128)(2,1)S(1)} %collective-permute-done.5, bf16[3072,4096]{1,0:T(8,128)(2,1)} %bitcast.40, s32[]{:T(128)S(6)} %select_n.27), kind=kOutput, calls=%fused_computation.25 | convolution fusion | flops 805699584 | bytes 9699332 | tf_op jit(solution)/shard_map/dot_general | solution.py:68
  58.1 0.0 slice-start.5
  58.1 4.8 %fusion.42 = bf16[3072,128]{1,0:T(8,128)(2,1)S(1)} fusion(f32[3072,128]{1,0:T(8,128)S(1)} %fusion.27, f32[16,128]{1,0:T(8,128)S(1)} %select_reduce_fusion, f32[3072,128]{1,0:T(8,128)S(1)} %fusion.36, bf16[128,1024]{1,0:T(8,128)(2,1)S(1)} %collective-permute-done.5, bf16[3072,4096]{1,0:T(8,128)(2,1)} %bitcast.36, s32[]{:T(128)S(6)} %select_n.27), kind=kOutput, calls=%fused_computation.31 | convolution fusion | flops 808452096 | bytes 10493956 | tf_op jit(solution)/shard_map/dot_general | solution.py:68
  62.9 0.0 slice-done
  62.9 0.0 slice-done.1
  62.9 0.0 slice-done.2
  62.9 0.0 slice-done.3
  62.9 0.0 slice-done.4
  62.9 0.0 slice-done.5
  63.0 1.0 %fusion.46 = bf16[128,1024]{1,0:T(8,128)(2,1)S(1)} fusion(bf16[3072,128]{1,0:T(8,128)(2,1)S(1)} %fusion.42, bf16[3072,4096]{1,0:T(8,128)(2,1)S(1)} %bitcast.29, s32[]{:T(128)S(6)} %select_n.27), kind=kOutput, calls=%fused_computation.33 | convolution fusion | flops 805437440 | bytes 7340036 | tf_op jit(solution)/shard_map/dot_general | solution.py:81
  64.0 0.5 collective-permute-start.10
  64.5 1.0 %fusion.43 = bf16[128,1024]{1,0:T(8,128)(2,1)S(1)} fusion(bf16[3072,128]{1,0:T(8,128)(2,1)S(1)} %fusion.42, bf16[3072,4096]{1,0:T(8,128)(2,1)S(1)} %bitcast.30, s32[]{:T(128)S(6)} %select_n.13), kind=kOutput, calls=%fused_computation.32 | convolution fusion | flops 805437440 | bytes 7340036 | tf_op jit(solution)/shard_map/dot_general | solution.py:81
  65.5 0.1 collective-permute-start.9
  65.6 0.0 collective-permute-done.10
  65.7 1.0 %add_convert_fusion = bf16[128,1024]{1,0:T(8,128)(2,1)S(1)} fusion(bf16[128,1024]{1,0:T(8,128)(2,1)S(1)} %collective-permute-done.10, bf16[3072,128]{1,0:T(8,128)(2,1)S(1)} %fusion.42, bf16[3072,4096]{1,0:T(8,128)(2,1)S(1)} %bitcast.31, s32[]{:T(128)S(6)} %select_n.26), kind=kOutput, calls=%fused_computation.35 | convolution fusion | flops 805699584 | bytes 7602180 | tf_op jit(solution)/shard_map/dot_general | solution.py:81
  66.7 1.6 %collective-permute-start.11 = (bf16[128,1024]{1,0:T(8,128)(2,1)S(1)}, bf16[128,1024]{1,0:T(8,128)(2,1)S(1)}, u32[]{:S(2)}, u32[]{:S(2)}) collective-permute-start(bf16[128,1024]{1,0:T(8,128)(2,1)S(1)} %add_convert_fusion), channel_id=1, source_target_pairs={{0,2},{1,3},{2,0},{3,1},{4,6},{5,7},{6,4},{7,5},{8,10},{9,11},{10,... | collective-permute-start | bytes 786440 | tf_op jit(solution)/shard_map/ppermute | solution.py:9
  68.2 1.0 %fusion.6 = f32[128,1024]{1,0:T(8,128)S(1)} fusion(bf16[3072,128]{1,0:T(8,128)(2,1)S(1)} %fusion.42, bf16[3072,4096]{1,0:T(8,128)(2,1)S(1)} %bitcast.32, s32[]{:T(128)S(6)} %select_n.12), kind=kOutput, calls=%fused_computation.6 | convolution fusion | flops 805306368 | bytes 7602180 | tf_op jit(solution)/shard_map/dot_general | solution.py:81
  69.3 0.0 collective-permute-done.9
  69.3 6.1 %collective-permute-done.11 = bf16[128,1024]{1,0:T(8,128)(2,1)S(1)} collective-permute-done((bf16[128,1024]{1,0:T(8,128)(2,1)S(1)}, bf16[128,1024]{1,0:T(8,128)(2,1)S(1)}, u32[]{:S(2)}, u32[]{:S(2)}) %collective-permute-start.11) | collective-permute-done | bytes 262176 | tf_op jit(solution)/shard_map/ppermute | solution.py:9
  75.4 0.1 fusion.67
  75.5 0.1 collective-permute-start.12
  75.6 0.6 collective-permute-start.13
  76.2 3.8 %collective-permute-start.14 = (bf16[32,1024]{1,0:T(8,128)(2,1)S(1)}, bf16[32,1024]{1,0:T(8,128)(2,1)S(1)}, u32[]{:S(2)}, u32[]{:S(2)}) collective-permute-start(bf16[32,1024]{1,0:T(8,128)(2,1)S(1)} %get-tuple-element.8), channel_id=1, source_target_pairs={{0,12},{4,8},{8,4},{12,0},{1,13},{5,9},{9,5},{13,1},{2,14},{6,10},... | collective-permute-start | bytes 196616 | tf_op jit(solution)/shard_map/ppermute | solution.py:9
  80.0 0.2 collective-permute-done.12
  80.1 3.5 %collective-permute-done.13 = bf16[32,1024]{1,0:T(8,128)(2,1)S(1)} collective-permute-done((bf16[32,1024]{1,0:T(8,128)(2,1)S(1)}, bf16[32,1024]{1,0:T(8,128)(2,1)S(1)}, u32[]{:S(2)}, u32[]{:S(2)}) %collective-permute-start.13) | collective-permute-done | bytes 65568 | tf_op jit(solution)/shard_map/ppermute | solution.py:9
  83.6 0.0 collective-permute-done.14
  83.7 0.7 fusion.51
  (9 shorter events, 0.1 us)
Async XLA Ops:
  0.0 13.3 %collective-permute-start = (bf16[32,1024]{1,0:T(8,128)(2,1)}, bf16[32,1024]{1,0:T(8,128)(2,1)S(1)}, u32[]{:S(2)}, u32[]{:S(2)}) collective-permute-start(bf16[32,1024]{1,0:T(8,128)(2,1)} %param.6), channel_id=1, source_target_pairs={{0,4},{4,0},{8,12},{12,8},{1,5},{5,1},{9,13},{13,9},{2,6},{6,2},{1... | collective-permute-start | bytes 196616 | tf_op jit(solution)/shard_map/ppermute | solution.py:9
  3.1 10.3 %collective-permute-start.1 = (bf16[32,1024]{1,0:T(8,128)(2,1)}, bf16[32,1024]{1,0:T(8,128)(2,1)S(1)}, u32[]{:S(2)}, u32[]{:S(2)}) collective-permute-start(bf16[32,1024]{1,0:T(8,128)(2,1)} %param.6), channel_id=1, source_target_pairs={{0,8},{4,12},{8,0},{12,4},{1,9},{5,13},{9,1},{13,5},{2,10},{6,14},... | collective-permute-start | bytes 196616 | tf_op jit(solution)/shard_map/ppermute | solution.py:9
  7.0 5.2 %collective-permute-start.6 = (s32[32,16]{0,1:T(8,128)S(1)}, s32[32,16]{0,1:T(8,128)S(1)}, u32[]{:S(2)}, u32[]{:S(2)}) collective-permute-start(s32[32,16]{0,1:T(8,128)S(1)} %constant_dynamic-update-slice_fusion.4), channel_id=1, source_target_pairs={{0,4},{4,0},{8,12},{12,8},{1,5},{5,1},{9,13},{13,9},{2,6},{6,2},{1... | collective-permute-start | bytes 6152 | tf_op jit(solution)/shard_map/ppermute | solution.py:9
  7.5 4.9 %collective-permute-start.7 = (s32[32,16]{0,1:T(8,128)S(1)}, s32[32,16]{0,1:T(8,128)S(1)}, u32[]{:S(2)}, u32[]{:S(2)}) collective-permute-start(s32[32,16]{0,1:T(8,128)S(1)} %constant_dynamic-update-slice_fusion.4), channel_id=1, source_target_pairs={{0,8},{4,12},{8,0},{12,4},{1,9},{5,13},{9,1},{13,5},{2,10},{6,14},... | collective-permute-start | bytes 6152 | tf_op jit(solution)/shard_map/ppermute | solution.py:9
  7.5 5.7 %collective-permute-start.8 = (s32[32,16]{0,1:T(8,128)S(1)}, s32[32,16]{0,1:T(8,128)S(1)}, u32[]{:S(2)}, u32[]{:S(2)}) collective-permute-start(s32[32,16]{0,1:T(8,128)S(1)} %constant_dynamic-update-slice_fusion.4), channel_id=1, source_target_pairs={{0,12},{4,8},{8,4},{12,0},{1,13},{5,9},{9,5},{13,1},{2,14},{6,10},... | collective-permute-start | bytes 6152 | tf_op jit(solution)/shard_map/ppermute | solution.py:9
  12.3 6.3 %collective-permute-start.2 = (bf16[32,1024]{1,0:T(8,128)(2,1)}, bf16[32,1024]{1,0:T(8,128)(2,1)S(1)}, u32[]{:S(2)}, u32[]{:S(2)}) collective-permute-start(bf16[32,1024]{1,0:T(8,128)(2,1)} %param.6), channel_id=1, source_target_pairs={{0,12},{4,8},{8,4},{12,0},{1,13},{5,9},{9,5},{13,1},{2,14},{6,10},... | collective-permute-start | bytes 196616 | tf_op jit(solution)/shard_map/ppermute | solution.py:9
  18.6 6.4 %collective-permute-start.4 = (bf16[128,1024]{1,0:T(8,128)(2,1)S(1)}, bf16[128,1024]{1,0:T(8,128)(2,1)S(1)}, u32[]{:S(2)}, u32[]{:S(2)}) collective-permute-start(bf16[128,1024]{1,0:T(8,128)(2,1)S(1)} %constant_dynamic-update-slice_fusion), channel_id=1, source_target_pairs={{0,2},{1,3},{2,0},{3,1},{4,6},{5,7},{6,4},{7,5},{8,10},{9,11},{10,... | collective-permute-start | bytes 786440 | tf_op jit(solution)/shard_map/ppermute | solution.py:9
  20.2 9.4 %collective-permute-start.3 = (bf16[128,1024]{1,0:T(8,128)(2,1)S(1)}, bf16[128,1024]{1,0:T(8,128)(2,1)S(1)}, u32[]{:S(2)}, u32[]{:S(2)}) collective-permute-start(bf16[128,1024]{1,0:T(8,128)(2,1)S(1)} %constant_dynamic-update-slice_fusion), channel_id=1, source_target_pairs={{0,1},{1,0},{2,3},{3,2},{4,5},{5,4},{6,7},{7,6},{8,9},{9,8},{10,11... | collective-permute-start | bytes 786440 | tf_op jit(solution)/shard_map/ppermute | solution.py:9
  38.8 14.4 %collective-permute-start.5 = (bf16[128,1024]{1,0:T(8,128)(2,1)S(1)}, bf16[128,1024]{1,0:T(8,128)(2,1)S(1)}, u32[]{:S(2)}, u32[]{:S(2)}) collective-permute-start(bf16[128,1024]{1,0:T(8,128)(2,1)S(1)} %collective-permute-done.4), channel_id=1, source_target_pairs={{0,1},{1,0},{2,3},{3,2},{4,5},{5,4},{6,7},{7,6},{8,9},{9,8},{10,11... | collective-permute-start | bytes 786440 | tf_op jit(solution)/shard_map/ppermute | solution.py:9
  38.8 24.0 %slice-start = ((s8[25165824]{0:T(1024)(128)(4,1)}), s8[4194304]{0:T(1024)(128)(4,1)S(1)}, s32[]{:S(2)}) async-start(s8[25165824]{0:T(1024)(128)(4,1)} %bitcast.27), calls=%async_computation | async-start | bytes 8388608
  38.9 24.0 %slice-start.1 = ((s8[25165824]{0:T(1024)(128)(4,1)}), s8[4194304]{0:T(1024)(128)(4,1)S(1)}, s32[]{:S(2)}) async-start(s8[25165824]{0:T(1024)(128)(4,1)} %bitcast.27), calls=%async_computation.1 | async-start | bytes 8388608
  43.6 19.3 %slice-start.2 = ((s8[25165824]{0:T(1024)(128)(4,1)}), s8[4194304]{0:T(1024)(128)(4,1)S(1)}, s32[]{:S(2)}) async-start(s8[25165824]{0:T(1024)(128)(4,1)} %bitcast.27), calls=%async_computation.2 | async-start | bytes 8388608
  48.4 14.5 %slice-start.3 = ((s8[25165824]{0:T(1024)(128)(4,1)}), s8[4194304]{0:T(1024)(128)(4,1)S(1)}, s32[]{:S(2)}) async-start(s8[25165824]{0:T(1024)(128)(4,1)} %bitcast.27), calls=%async_computation.3 | async-start | bytes 8388608
  53.1 9.8 %slice-start.4 = ((s8[25165824]{0:T(1024)(128)(4,1)}), s8[4194304]{0:T(1024)(128)(4,1)S(1)}, s32[]{:S(2)}) async-start(s8[25165824]{0:T(1024)(128)(4,1)} %bitcast.27), calls=%async_computation.4 | async-start | bytes 8388608
  58.1 4.8 %slice-start.5 = ((s8[25165824]{0:T(1024)(128)(4,1)}), s8[4194304]{0:T(1024)(128)(4,1)S(1)}, s32[]{:S(2)}) async-start(s8[25165824]{0:T(1024)(128)(4,1)} %bitcast.27), calls=%async_computation.5 | async-start | bytes 8388608
  64.0 1.7 %collective-permute-start.10 = (bf16[128,1024]{1,0:T(8,128)(2,1)S(1)}, bf16[128,1024]{1,0:T(8,128)(2,1)S(1)}, u32[]{:S(2)}, u32[]{:S(2)}) collective-permute-start(bf16[128,1024]{1,0:T(8,128)(2,1)S(1)} %fusion.46), channel_id=1, source_target_pairs={{0,1},{1,0},{2,3},{3,2},{4,5},{5,4},{6,7},{7,6},{8,9},{9,8},{10,11... | collective-permute-start | bytes 786440 | tf_op jit(solution)/shard_map/ppermute | solution.py:9
  65.5 3.7 %collective-permute-start.9 = (bf16[128,1024]{1,0:T(8,128)(2,1)S(1)}, bf16[128,1024]{1,0:T(8,128)(2,1)S(1)}, u32[]{:S(2)}, u32[]{:S(2)}) collective-permute-start(bf16[128,1024]{1,0:T(8,128)(2,1)S(1)} %fusion.43), channel_id=1, source_target_pairs={{0,1},{1,0},{2,3},{3,2},{4,5},{5,4},{6,7},{7,6},{8,9},{9,8},{10,11... | collective-permute-start | bytes 786440 | tf_op jit(solution)/shard_map/ppermute | solution.py:9
  66.7 8.7 %collective-permute-start.11 = (bf16[128,1024]{1,0:T(8,128)(2,1)S(1)}, bf16[128,1024]{1,0:T(8,128)(2,1)S(1)}, u32[]{:S(2)}, u32[]{:S(2)}) collective-permute-start(bf16[128,1024]{1,0:T(8,128)(2,1)S(1)} %add_convert_fusion), channel_id=1, source_target_pairs={{0,2},{1,3},{2,0},{3,1},{4,6},{5,7},{6,4},{7,5},{8,10},{9,11},{10,... | collective-permute-start | bytes 786440 | tf_op jit(solution)/shard_map/ppermute | solution.py:9
  75.5 4.6 %collective-permute-start.12 = (bf16[32,1024]{1,0:T(8,128)(2,1)S(1)}, bf16[32,1024]{1,0:T(8,128)(2,1)S(1)}, u32[]{:S(2)}, u32[]{:S(2)}) collective-permute-start(bf16[32,1024]{1,0:T(8,128)(2,1)S(1)} %get-tuple-element.7), channel_id=1, source_target_pairs={{0,4},{4,0},{8,12},{12,8},{1,5},{5,1},{9,13},{13,9},{2,6},{6,2},{1... | collective-permute-start | bytes 196616 | tf_op jit(solution)/shard_map/ppermute | solution.py:9
  75.6 8.0 %collective-permute-start.13 = (bf16[32,1024]{1,0:T(8,128)(2,1)S(1)}, bf16[32,1024]{1,0:T(8,128)(2,1)S(1)}, u32[]{:S(2)}, u32[]{:S(2)}) collective-permute-start(bf16[32,1024]{1,0:T(8,128)(2,1)S(1)} %get-tuple-element.9), channel_id=1, source_target_pairs={{0,8},{4,12},{8,0},{12,4},{1,9},{5,13},{9,1},{13,5},{2,10},{6,14},... | collective-permute-start | bytes 196616 | tf_op jit(solution)/shard_map/ppermute | solution.py:9
  76.2 7.5 %collective-permute-start.14 = (bf16[32,1024]{1,0:T(8,128)(2,1)S(1)}, bf16[32,1024]{1,0:T(8,128)(2,1)S(1)}, u32[]{:S(2)}, u32[]{:S(2)}) collective-permute-start(bf16[32,1024]{1,0:T(8,128)(2,1)S(1)} %get-tuple-element.8), channel_id=1, source_target_pairs={{0,12},{4,8},{8,4},{12,0},{1,13},{5,9},{9,5},{13,1},{2,14},{6,10},... | collective-permute-start | bytes 196616 | tf_op jit(solution)/shard_map/ppermute | solution.py:9
